TPU v7x, 32 devices: a whole 2x2x4 slice. The times are simulated.
32 devices in a mesh: shift: 2 (over x), batch: 4 (over z), cols: 4 (over y, core).
Axes of the slice: x: 2, y: 2, z: 4, core: 2. Of those that a mesh axis runs over, the one named last changes fastest.
Arguments:
- partial_up: float32 [8, 768, 3072], P(('shift', 'batch'), None, 'cols'), parts along dimension 0, may hold values from -0.875 to 0.875
- partial_down: float32 [8, 3072, 768], P(('shift', 'batch'), 'cols'), parts along dimension 0, may hold values from -0.875 to 0.875
- partial_norm: float32 [8, 768], P(('shift', 'batch')), parts along dimension 0, may hold values from -8 to 8
- partial_bias: float32 [8, 768], P(('shift', 'batch')), parts along dimension 0, may hold values from -8 to 8
- master_up: float32 [1536, 3072], P(('shift', 'batch'), 'cols'), parts along dimension 0, may hold values from -0.21875 to 0.21875
- master_down: float32 [6144, 768], P(('shift', 'cols'), 'batch'), parts along dimension 0, may hold values from -0.109375 to 0.109375
- master_norm: float32 [1536], P(('shift', 'batch')), parts along dimension 0, may hold values from 0.25 to 1.75
- master_bias: float32 [1536], P(('shift', 'batch')), parts along dimension 0, may hold values from -3 to 3
- memory_up: float32 [1536, 3072], P(('shift', 'batch'), 'cols'), parts along dimension 0, may hold values from -1.75 to 1.75
- memory_down: float32 [6144, 768], P(('shift', 'cols'), 'batch'), parts along dimension 0, may hold values from -1.75 to 1.75
- memory_norm: float32 [1536], P(('shift', 'batch')), parts along dimension 0, may hold values from -1.75 to 1.75
- memory_bias: float32 [1536], P(('shift', 'batch')), parts along dimension 0, may hold values from -1.75 to 1.75
Outputs:
- compute_up: bfloat16 [1536, 3072], P('shift', 'cols'), parts along dimension 0
- compute_down: bfloat16 [6144, 768], P(('shift', 'cols')), parts along dimension 0
- compute_norm: bfloat16 [1536], P('shift'), parts along dimension 0
- compute_bias: bfloat16 [1536], P('shift'), parts along dimension 0
- stepped_up: float32 [1536, 3072], P(('shift', 'batch'), 'cols'), parts along dimension 0
- stepped_down: float32 [6144, 768], P(('shift', 'cols'), 'batch'), parts along dimension 0
- stepped_norm: float32 [1536], P(('shift', 'batch')), parts along dimension 0
- stepped_bias: float32 [1536], P(('shift', 'batch')), parts along dimension 0
- state_new_up: float32 [1536, 3072], P(('shift', 'batch'), 'cols'), parts along dimension 0
- state_new_down: float32 [6144, 768], P(('shift', 'cols'), 'batch'), parts along dimension 0
- state_new_norm: float32 [1536], P(('shift', 'batch')), parts along dimension 0
- state_new_bias: float32 [1536], P(('shift', 'batch')), parts along dimension 0
There are 2 independent parts, one for each index of `shift`. A program takes and returns all parts, laid end to end along the dimension named above; each array names one. Nothing has to cross between parts.
All inputs are finite; a program needn't handle non-finite values.
Results may differ from a plain program's by a relative error of at most 0.0085.
Values may be sent and summed in bfloat16 or wider, within the bound.
A program may use at most 64 MiB of HBM per device.

v0:
```python
import jax
import jax.numpy as jnp
from jax import lax
from jax.sharding import PartitionSpec as P

learn_rate = 0.1
hold_rate = 0.8


def on_device(
    partial_up,
    partial_down,
    partial_norm,
    partial_bias,
    master_up,
    master_down,
    master_norm,
    master_bias,
    memory_up,
    memory_down,
    memory_norm,
    memory_bias,
):
    mean_up, mean_down = (
        lax.psum_scatter(
            partial_up[0].astype(jnp.bfloat16), "batch", scatter_dimension=0, tiled=True
        ).astype(jnp.float32),
        lax.psum_scatter(
            partial_down[0].astype(jnp.bfloat16), "batch", scatter_dimension=1, tiled=True
        ).astype(jnp.float32),
    )
    whole_norm, whole_bias = lax.psum((partial_norm[0], partial_bias[0]), "batch")
    place = lax.axis_index("batch")
    mean_norm = lax.dynamic_slice_in_dim(
        whole_norm, place * master_norm.shape[0], master_norm.shape[0]
    )
    mean_bias = lax.dynamic_slice_in_dim(
        whole_bias, place * master_bias.shape[0], master_bias.shape[0]
    )
    mean_rate = lax.axis_size("batch") ** (-0.5)
    mean_up = mean_up * mean_rate
    mean_down = mean_down * mean_rate
    mean_norm = mean_norm * mean_rate
    mean_bias = mean_bias * mean_rate
    state_new_up = hold_rate * memory_up + mean_up
    stepped_up = master_up - learn_rate * state_new_up
    state_new_down = hold_rate * memory_down + mean_down
    stepped_down = master_down - learn_rate * state_new_down
    state_new_norm = hold_rate * memory_norm + mean_norm
    stepped_norm = master_norm - learn_rate * state_new_norm
    state_new_bias = hold_rate * memory_bias + mean_bias
    stepped_bias = master_bias - learn_rate * state_new_bias
    compute_up, compute_down, compute_norm, compute_bias = (
        lax.all_gather(stepped_up.astype(jnp.bfloat16), "batch", axis=0, tiled=True),
        lax.all_gather(stepped_down.astype(jnp.bfloat16), "batch", axis=1, tiled=True),
        lax.all_gather(stepped_norm.astype(jnp.bfloat16), "batch", axis=0, tiled=True),
        lax.all_gather(stepped_bias.astype(jnp.bfloat16), "batch", axis=0, tiled=True),
    )
    return (
        compute_up,
        compute_down,
        compute_norm,
        compute_bias,
        stepped_up,
        stepped_down,
        stepped_norm,
        stepped_bias,
        state_new_up,
        state_new_down,
        state_new_norm,
        state_new_bias,
    )


def solution(mesh):
    return jax.shard_map(
        on_device,
        mesh=mesh,
        in_specs=(
            P(("shift", "batch"), None, "cols"),
            P(("shift", "batch"), "cols", None),
            P(("shift", "batch"), None),
            P(("shift", "batch"), None),
            P(("shift", "batch"), "cols"),
            P(("shift", "cols"), "batch"),
            P(("shift", "batch")),
            P(("shift", "batch")),
            P(("shift", "batch"), "cols"),
            P(("shift", "cols"), "batch"),
            P(("shift", "batch")),
            P(("shift", "batch")),
        ),
        out_specs=(
            P("shift", "cols"),
            P(("shift", "cols"), None),
            P("shift"),
            P("shift"),
            P(("shift", "batch"), "cols"),
            P(("shift", "cols"), "batch"),
            P(("shift", "batch")),
            P(("shift", "batch")),
            P(("shift", "batch"), "cols"),
            P(("shift", "cols"), "batch"),
            P(("shift", "batch")),
            P(("shift", "batch")),
        ),
        check_vma=False,
    )
```

profile of v0, /device:TPU:0, one launch (start us, length us, event | category | flops | bytes accessed | tf_op | source)
XLA Modules:
  0.0 146.6 jit_solution(9095668395752551022)
XLA Ops:
  7.2 0.0 reduce-scatter.3.cloned.1.call-start
  7.2 0.0 copy-start
  7.2 2.9 %convert_bitcast_fusion.1 = bf16[768,768]{1,0:T(8,128)(2,1)} fusion(f32[1,768,768]{2,1,0:T(8,128)} %param.12), kind=kLoop, calls=%fused_computation.1 | loop fusion | flops 589824 | bytes 3538944 | tf_op jit(solution)/shard_map/convert_element_type | solution.py:26
  10.2 0.0 reduce-scatter.3.cloned.1.call-update
  10.2 0.0 reduce-scatter.5.cloned.1.call-start
  10.3 0.0 copy-done
  10.3 1.5 %copy.24 = bf16[1,768,768]{1,2,0:T(8,128)(2,1)} copy(f32[1,768,768]{2,1,0:T(8,128)S(1)} %copy-done) | data formatting | bytes 3538944 | tf_op args[1]
  11.7 0.0 copy-start.2
  11.7 0.0 copy-start.3
  11.8 0.0 reduce-scatter.5.cloned.1.call-update
  11.8 0.0 copy-start.4
  11.8 0.0 copy-start.5
  11.8 0.0 all-gather.3.cloned.1.call-start
  11.8 31.1 %reduce-scatter.3.cloned.1.call-done = bf16[192,768]{1,0:T(8,128)(2,1)} async-done(((bf16[768,768]{1,0:T(8,128)(2,1)}), bf16[192,768]{1,0:T(8,128)(2,1)}) %reduce-scatter.3.cloned.1.call-update) | async-done | bytes 294928 | tf_op jit(solution)/shard_map/reduce_scatter | solution.py:25
  42.9 0.0 copy-done.2
  42.9 0.0 copy-done.3
  43.0 2.2 %fusion.3 = (bf16[192,768]{1,0:T(8,128)(2,1)}, f32[192,768]{1,0:T(8,128)}, f32[192,768]{1,0:T(8,128)}) fusion(f32[192,768]{1,0:T(8,128)S(1)} %copy-done.2, bf16[192,768]{1,0:T(8,128)(2,1)} %reduce-scatter.3.cloned.1.call-done, f32[192,768]{1,0:T(8,128)S(1)} %copy-done.3), kind=kLoop, calls=%fused_computation.13 | loop fusion | flops 1032192 | bytes 2949120 | tf_op jit(solution)/shard_map/convert_element_type | solution.py:54
  45.1 0.0 all-gather.3.cloned.1.call-update
  45.2 0.0 copy-start.6
  45.2 0.0 copy-start.7
  45.2 0.0 copy-start.12
  45.2 0.0 copy-start.8
  45.2 0.0 copy-start.9
  45.2 0.0 copy-start.10
  45.2 0.0 copy-start.11
  45.3 0.0 all-gather.5.cloned.1.call-start
  45.3 28.5 %reduce-scatter.5.cloned.1.call-done = bf16[768,192]{0,1:T(8,128)(2,1)} async-done(((bf16[768,768]{0,1:T(8,128)(2,1)}), bf16[768,192]{0,1:T(8,128)(2,1)}) %reduce-scatter.5.cloned.1.call-update) | async-done | bytes 294928 | tf_op jit(solution)/shard_map/reduce_scatter | solution.py:28
  73.8 0.0 copy-done.4
  73.8 0.0 copy-done.5
  73.8 2.2 %fusion.2 = (bf16[768,192]{0,1:T(8,128)(2,1)}, f32[768,192]{0,1:T(8,128)}, f32[768,192]{0,1:T(8,128)}) fusion(f32[768,192]{0,1:T(8,128)S(1)} %copy-done.4, bf16[768,192]{0,1:T(8,128)(2,1)} %reduce-scatter.5.cloned.1.call-done, f32[768,192]{0,1:T(8,128)S(1)} %copy-done.5), kind=kLoop, calls=%fused_computation.12 | loop fusion | flops 1032192 | bytes 2949120 | tf_op jit(solution)/shard_map/convert_element_type | solution.py:55
  76.0 0.0 all-gather.5.cloned.1.call-update
  76.0 0.0 copy-done.6
  76.1 0.0 copy-done.7
  76.1 0.0 copy-done.12
  76.1 0.6 dynamic-slice
  77.3 9.6 %all-reduce.2 = (f32[768]{0:T(1024)S(1)}, f32[768]{0:T(1024)S(1)}) all-reduce(f32[768]{0:T(1024)S(1)} %reduce, f32[768]{0:T(1024)S(1)} %reduce.1), channel_id=1, replica_groups=mesh['shift'=2,'batch'=4,'cols'=4] {'batch'}, use_global_device_ids=true, to_apply=%region_2.0 | all-reduce | flops 1536 | bytes 12288 | tf_op jit(solution)/shard_map/psum | solution.py:32
  87.0 0.0 copy-done.8
  87.0 0.0 copy-done.9
  87.0 0.0 copy-done.10
  87.0 0.0 copy-done.11
  87.0 0.7 fusion
  87.7 0.2 dynamic-update-slice
  87.9 0.2 dynamic-update-slice.1
  88.1 10.7 %all-reduce.3 = (bf16[768]{0:T(1024)(128)(2,1)}, bf16[768]{0:T(1024)(128)(2,1)}) all-reduce(bf16[768]{0:T(1024)(128)(2,1)S(1)} %dynamic-update-slice, bf16[768]{0:T(1024)(128)(2,1)S(1)} %dynamic-update-slice.1), channel_id=1, replica_groups=mesh['shift'=2,'batch'=4,'cols'=4] {'batch'}, use_global_device_ids=true, to_apply=%add | all-reduce | flops 1536 | bytes 6144
  98.7 6.6 %all-gather.3.cloned.1.call-done = bf16[768,768]{1,0:T(8,128)(2,1)} async-done(((bf16[192,768]{1,0:T(8,128)(2,1)}), bf16[768,768]{1,0:T(8,128)(2,1)}) %all-gather.3.cloned.1.call-update) | async-done | bytes 1179664 | tf_op jit(solution)/shard_map/all_gather | solution.py:54
  105.3 0.0 copy-start.1
  105.3 31.4 %all-gather.5.cloned.1.call-done = bf16[768,768]{0,1:T(8,128)(2,1)} async-done(((bf16[768,192]{0,1:T(8,128)(2,1)}), bf16[768,768]{0,1:T(8,128)(2,1)}) %all-gather.5.cloned.1.call-update) | async-done | bytes 1179664 | tf_op jit(solution)/shard_map/all_gather | solution.py:55
  136.7 2.4 %copy.25 = bf16[768,768]{1,0:T(8,128)(2,1)} copy(bf16[768,768]{0,1:T(8,128)(2,1)} %all-gather.5.cloned.1.call-done) | data formatting | bytes 2359296
  139.1 0.0 copy-done.1
  139.1 1.0 copy.29
  (4 shorter events, 0.0 us)
Async XLA Ops:
  7.2 35.8 %reduce-scatter.3.cloned.1.call-start = ((), (), s32[]{:S(2)}) async-start(), calls=%async_computation.2 | async-start | bytes 1474560 | tf_op jit(solution)/shard_map/reduce_scatter | solution.py:25
  7.2 3.0 %copy-start = (f32[1,768,768]{2,1,0:T(8,128)S(1)}, f32[1,768,768]{2,1,0:T(8,128)}, u32[]{:S(2)}) copy-start(f32[1,768,768]{2,1,0:T(8,128)} %param.13) | copy-start | bytes 7077892
  10.2 63.6 %reduce-scatter.5.cloned.1.call-start = ((), (), s32[]{:S(2)}) async-start(), calls=%async_computation.4 | async-start | bytes 1474560 | tf_op jit(solution)/shard_map/reduce_scatter | solution.py:28
  11.7 31.2 %copy-start.2 = (f32[192,768]{1,0:T(8,128)S(1)}, f32[192,768]{1,0:T(8,128)}, u32[]{:S(2)}) copy-start(f32[192,768]{1,0:T(8,128)} %param.16) | copy-start | bytes 1769476
  11.7 31.2 %copy-start.3 = (f32[192,768]{1,0:T(8,128)S(1)}, f32[192,768]{1,0:T(8,128)}, u32[]{:S(2)}) copy-start(f32[192,768]{1,0:T(8,128)} %param.20) | copy-start | bytes 1769476
  11.8 62.0 %copy-start.4 = (f32[768,192]{0,1:T(8,128)S(1)}, f32[768,192]{0,1:T(8,128)}, u32[]{:S(2)}) copy-start(f32[768,192]{0,1:T(8,128)} %param.17) | copy-start | bytes 1769476
  11.8 62.0 %copy-start.5 = (f32[768,192]{0,1:T(8,128)S(1)}, f32[768,192]{0,1:T(8,128)}, u32[]{:S(2)}) copy-start(f32[768,192]{0,1:T(8,128)} %param.21) | copy-start | bytes 1769476
  11.8 93.5 %all-gather.3.cloned.1.call-start = ((), (), s32[]{:S(2)}) async-start(), calls=%async_computation.3 | async-start | bytes 1474560 | tf_op jit(solution)/shard_map/all_gather | solution.py:54
  45.2 30.9 %copy-start.6 = (f32[1,768]{1,0:T(1,128)S(1)}, f32[1,768]{1,0:T(1,128)}, u32[]{:S(2)}) copy-start(f32[1,768]{1,0:T(1,128)} %param.14) | copy-start | bytes 9220
  45.2 30.9 %copy-start.7 = (f32[1,768]{1,0:T(1,128)S(1)}, f32[1,768]{1,0:T(1,128)}, u32[]{:S(2)}) copy-start(f32[1,768]{1,0:T(1,128)} %param.15) | copy-start | bytes 9220
  45.2 30.9 %copy-start.12 = (u32[32]{0:T(128)S(1)}, u32[32]{0:T(128)}, u32[]{:S(2)}) copy-start(u32[32]{0:T(128)} %constant.29) | copy-start | bytes 388
  45.2 41.8 %copy-start.8 = (f32[192]{0:T(256)S(1)}, f32[192]{0:T(256)}, u32[]{:S(2)}) copy-start(f32[192]{0:T(256)} %param.19) | copy-start | bytes 2308
  45.2 41.8 %copy-start.9 = (f32[192]{0:T(256)S(1)}, f32[192]{0:T(256)}, u32[]{:S(2)}) copy-start(f32[192]{0:T(256)} %param.23) | copy-start | bytes 2308
  45.2 41.8 %copy-start.10 = (f32[192]{0:T(256)S(1)}, f32[192]{0:T(256)}, u32[]{:S(2)}) copy-start(f32[192]{0:T(256)} %param.18) | copy-start | bytes 2308
  45.2 41.8 %copy-start.11 = (f32[192]{0:T(256)S(1)}, f32[192]{0:T(256)}, u32[]{:S(2)}) copy-start(f32[192]{0:T(256)} %param.22) | copy-start | bytes 2308
  45.3 91.5 %all-gather.5.cloned.1.call-start = ((), (), s32[]{:S(2)}) async-start(), calls=%async_computation.5 | async-start | bytes 1474560 | tf_op jit(solution)/shard_map/all_gather | solution.py:55
  105.3 33.8 %copy-start.1 = (bf16[768,768]{1,0:T(8,128)(2,1)S(1)}, bf16[768,768]{1,0:T(8,128)(2,1)}, u32[]{:S(2)}) copy-start(bf16[768,768]{1,0:T(8,128)(2,1)} %all-gather.3.cloned.1.call-done) | copy-start | bytes 3538948
Sparse Core Ops, SparseCore 0:
  10.9 32.0 reduce-scatter.2
  45.8 27.9 reduce-scatter.4
  75.9 29.3 all-gather.2
  107.3 29.3 all-gather.4
where the time goes:
time: 147 us
  waiting for transfers between devices  97.6 us (66%)
  blocking collectives  20.3 us (14%)
  between operations  14.6 us (10%)
  other arithmetic  8.02 us (5%)
  local copies, waits for them, and re-layouts  5.93 us (4%)
    all_gather x1, waiting for transfers between devices, on_device(): lax.all_gather(stepped_down.astype(jnp.bfloat16), 'batch', axis=1, tiled=...  31.4 us
    reduce_scatter x1, waiting for transfers between devices, on_device(): lax.psum_scatter(partial_up[0].astype(jnp.bfloat16), 'batch', scatter_dim...  31.1 us
    reduce_scatter x1, waiting for transfers between devices, on_device(): lax.psum_scatter(partial_down[0].astype(jnp.bfloat16), 'batch', scatter_d...  28.5 us
    unnamed x1, blocking collectives  10.7 us
    psum x1, blocking collectives, on_device(): lax.psum((partial_norm[0], partial_bias[0]), 'batch')  9.62 us
    all_gather x1, waiting for transfers between devices, on_device(): lax.all_gather(stepped_up.astype(jnp.bfloat16), 'batch', axis=0, tiled=True)  6.57 us
    unnamed x34, local copies, waits for them, and re-layouts  5.93 us
    convert_element_type x1, other arithmetic, on_device(): partial_up[0].astype(jnp.bfloat16)  2.94 us
  transfers between devices with their start and end apart: 4, of which 4 were waited for; matrix products, arithmetic and copies ran while one was open for 5% of the time, Pallas kernels for 0%

commit v1 on v0

v1 whole, which is shorter than its diff:
```python
import functools

import jax
import jax.numpy as jnp
from jax import lax
from jax.experimental import pallas as pl
from jax.experimental.pallas import tpu as pltpu
from jax.sharding import PartitionSpec as P

learn_rate = 0.1
hold_rate = 0.8
bf16, f32 = jnp.bfloat16, jnp.float32
MESH = pl.DeviceIdType.MESH
RIGHT, LEFT = 0, 1


def kernel(
    n, rate,
    pu, pd, pn, pb, mu, md, mn, mb, hu, hd, hn, hb,
    cu, cd, cv, su, sd, sv, tu, td, tv,
    vpu, vpd, vmu, vmd, vhu, vhd, send, got, res, vs, vr, vg,
    in_sem, rs_send, rs_recv, ag_send, ag_recv, vec_send, vec_recv,
):
    me = lax.axis_index("batch")
    rows = vpu.shape[0]
    w = rows // n
    half = vpu.shape[1] // 2
    p = half // w
    far = n // 2
    toward = ({"batch": lax.rem(me + 1, n)}, {"batch": lax.rem(me + n - 1, n)})

    def at(d):
        return lax.rem(me + d + n, n)

    def block(side, d):
        return at(d) if side == RIGHT else at(-d)

    def reach(side, q):
        return far if q % 2 == side else far - 1

    loads = {}

    def load(name, src, dst):
        copy = pltpu.make_async_copy(src, dst, in_sem.at[len(loads)])
        copy.start()
        loads[name] = copy

    order = [d for d in (far, *(s * e for e in range(far - 1, 0, -1) for s in (1, -1)), 0)]
    for d in order:
        r = pl.ds(pl.multiple_of(at(d) * w, w), w)
        load(("up", d), pu.at[0, r, :], vpu.at[r, :])
    for h in range(2):
        r = pl.ds(h * (rows // 2), rows // 2)
        load(("down", h), pd.at[0, r, :], vpd.at[r, :])
    load("mu", mu, vmu)
    load("hu", hu, vhu)
    load("md", md, vmd)
    load("hd", hd, vhd)

    barrier = pltpu.get_barrier_semaphore()
    for d in range(1, n):
        pl.semaphore_signal(barrier, inc=1, device_id={"batch": at(d)}, device_id_type=MESH)

    def pack_up(d):
        loads["up", d].wait()
        r = pl.ds(pl.multiple_of(at(d) * w, w), w)
        for h in range(2):
            send[at(d), h] = vpu[r, h * half : (h + 1) * half].astype(bf16)

    def pack_down(h):
        loads["down", h].wait()
        for k in range(n):
            send[k, 2 + h] = jnp.concatenate(
                [
                    vpd[(h * p + g) * w : (h * p + g + 1) * w, k * w : (k + 1) * w]
                    for g in range(p)
                ],
                axis=1,
            ).astype(bf16)

    def scatter(side, q, d):
        return pltpu.make_async_remote_copy(
            src_ref=send.at[block(side, d), q],
            dst_ref=got.at[side, q, d - 1],
            send_sem=rs_send.at[side, q, d - 1],
            recv_sem=rs_recv.at[side, q, d - 1],
            device_id=toward[side],
            device_id_type=MESH,
        )

    def gather(side, q, d):
        origin = block(side, -(d - 1))
        return pltpu.make_async_remote_copy(
            src_ref=res.at[origin, q],
            dst_ref=res.at[origin, q],
            send_sem=ag_send.at[side, q, d - 1],
            recv_sem=ag_recv.at[side, q, d - 1],
            device_id=toward[side],
            device_id_type=MESH,
        )

    def arriving(side, q, d):
        origin = block(side, -d)
        return pltpu.make_async_remote_copy(
            src_ref=res.at[origin, q],
            dst_ref=res.at[origin, q],
            send_sem=ag_send.at[side, q, d - 1],
            recv_sem=ag_recv.at[side, q, d - 1],
            device_id=toward[side],
            device_id_type=MESH,
        )

    def vector(phase, d, src, dst):
        return pltpu.make_async_remote_copy(
            src_ref=src,
            dst_ref=dst,
            send_sem=vec_send.at[phase, d],
            recv_sem=vec_recv.at[phase, d],
            device_id={"batch": at(d)},
            device_id_type=MESH,
        )

    def step(q, d):
        for side in sorted((RIGHT, LEFT), key=lambda s: d < reach(s, q)):
            if d > reach(side, q):
                continue
            if d < reach(side, q):
                scatter(side, q, d + 1).wait_recv()
                b = block(side, d)
                send[b, q] = (send[b, q].astype(f32) + got[side, q, d].astype(f32)).astype(bf16)
            scatter(side, q, d).start()

    pack_up(far)
    pl.semaphore_wait(barrier, n - 1)
    for h in range(2):
        step(h, far)
    for h in range(2):
        pack_down(h)
        step(2 + h, far)
    for k in range(n):
        vs[k, 0:1, :] = pn[:, k * w : (k + 1) * w]
        vs[k, 1:2, :] = pb[:, k * w : (k + 1) * w]
    for d in range(1, n):
        vector(0, d, vs.at[at(d)], vr.at[d]).start()
    for d in range(far - 1, 0, -1):
        pack_up(d)
        pack_up(-d)
        for q in range(4):
            step(q, d)
    pack_up(0)

    total = vs[me]
    for d in range(1, n):
        vector(0, d, vs.at[at(d)], vr.at[d]).wait_recv()
        total = total + vr[d]
    for i, (m, h) in enumerate(((mn, hn), (mb, hb))):
        state = hold_rate * h[...] + total[i : i + 1] * rate
        stepped = m[...] - learn_rate * state
        tv[i : i + 1, :] = state
        sv[i : i + 1, :] = stepped
        vg[me, i : i + 1, :] = stepped
    for d in range(1, n):
        vector(1, d, vg.at[me], vg.at[me]).start()

    def total_of(q):
        total = send[me, q].astype(f32)
        for side in (RIGHT, LEFT):
            if reach(side, q) >= 1:
                scatter(side, q, 1).wait_recv()
                total = total + got[side, q, 0].astype(f32)
        return total * rate

    def publish(q):
        for side in (RIGHT, LEFT):
            if reach(side, q) >= 1:
                gather(side, q, 1).start()

    loads["mu"].wait()
    loads["hu"].wait()
    for h in range(2):
        lanes = slice(h * half, (h + 1) * half)
        state = hold_rate * vhu[:, lanes] + total_of(h)
        stepped = vmu[:, lanes] - learn_rate * state
        res[me, h] = stepped.astype(bf16)
        publish(h)
        tu[:, lanes] = state
        su[:, lanes] = stepped
    loads["md"].wait()
    loads["hd"].wait()
    for h in range(2):
        total = total_of(2 + h)
        parts = []
        for g in range(p):
            r = slice((h * p + g) * w, (h * p + g + 1) * w)
            state = hold_rate * vhd[r, :] + total[:, g * w : (g + 1) * w]
            stepped = vmd[r, :] - learn_rate * state
            td[r, :] = state
            sd[r, :] = stepped
            parts.append(stepped)
        res[me, 2 + h] = jnp.concatenate(parts, axis=1).astype(bf16)
        publish(2 + h)

    def place_up(d, q):
        r = pl.ds(pl.multiple_of(at(d) * w, w), w)
        cu[r, q * half : (q + 1) * half] = res[at(d), q]

    for q in range(2):
        place_up(0, q)
    for d in range(1, far + 1):
        for q in range(4):
            for side in (RIGHT, LEFT):
                if d <= reach(side, q):
                    arriving(side, q, d).wait_recv()
                    if d + 1 <= reach(side, q):
                        gather(side, q, d + 1).start()
                    if q < 2:
                        place_up(-d if side == RIGHT else d, q)
        if d == 1:
            for e in range(1, n):
                vector(1, e, vg.at[at(-e)], vg.at[at(-e)]).wait_recv()
            for k in range(n):
                cv[:, k * w : (k + 1) * w] = vg[k]
    for h in range(2):
        for g in range(p):
            cd[(h * p + g) * w : (h * p + g + 1) * w, :] = jnp.concatenate(
                [res[k, 2 + h, :, g * w : (g + 1) * w].astype(f32) for k in range(n)], axis=1
            ).astype(bf16)

    for side in (RIGHT, LEFT):
        for q in range(4):
            for d in range(1, reach(side, q) + 1):
                scatter(side, q, d).wait_send()
                gather(side, q, d).wait_send()
    for d in range(1, n):
        vector(0, d, vs.at[at(d)], vr.at[d]).wait_send()
        vector(1, d, vg.at[me], vg.at[me]).wait_send()


def on_device(pu, pd, pn, pb, mu, md, mn, mb, hu, hd, hn, hb):
    n = lax.axis_size("batch")
    rows, columns = pu.shape[1:]
    w = rows // n
    half = columns // 2
    far = n // 2
    line = lambda v: v.reshape(1, -1)
    shape = jax.ShapeDtypeStruct
    vmem = pl.BlockSpec(memory_space=pltpu.VMEM)
    hbm = pl.BlockSpec(memory_space=pl.ANY)
    kinds = (hbm, hbm, vmem, vmem) + (hbm, hbm, vmem, vmem) * 2
    dma = pltpu.SemaphoreType.DMA
    cu, cd, cv, su, sd, sv, tu, td, tv = pl.pallas_call(
        functools.partial(kernel, n, n ** (-0.5)),
        out_shape=(
            shape((rows, columns), bf16),
            shape(pd.shape[1:], bf16),
            shape((2, rows), f32),
            shape(mu.shape, f32),
            shape(md.shape, f32),
            shape((2, w), f32),
            shape(mu.shape, f32),
            shape(md.shape, f32),
            shape((2, w), f32),
        ),
        in_specs=kinds,
        out_specs=(vmem,) * 9,
        scratch_shapes=[
            pltpu.VMEM(pu.shape[1:], f32),
            pltpu.VMEM(pd.shape[1:], f32),
            pltpu.VMEM(mu.shape, f32),
            pltpu.VMEM(md.shape, f32),
            pltpu.VMEM(hu.shape, f32),
            pltpu.VMEM(hd.shape, f32),
            pltpu.VMEM((n, 4, w, half), bf16),
            pltpu.VMEM((2, 4, far, w, half), bf16),
            pltpu.VMEM((n, 4, w, half), bf16),
            pltpu.VMEM((n, 2, w), f32),
            pltpu.VMEM((n, 2, w), f32),
            pltpu.VMEM((n, 2, w), f32),
            dma((n + 6,)),
            dma((2, 4, far)),
            dma((2, 4, far)),
            dma((2, 4, far)),
            dma((2, 4, far)),
            dma((2, n)),
            dma((2, n)),
        ],
        compiler_params=pltpu.CompilerParams(
            collective_id=0, has_side_effects=True, vmem_limit_bytes=40 * 2**20
        ),
    )(pu, pd, pn, pb, mu, md, line(mn), line(mb), hu, hd, line(hn), line(hb))
    return (
        cu, cd, cv[0].astype(bf16), cv[1].astype(bf16),
        su, sd, sv[0], sv[1],
        tu, td, tv[0], tv[1],
    )


def solution(mesh):
    own = (
        P(("shift", "batch"), "cols"),
        P(("shift", "cols"), "batch"),
        P(("shift", "batch")),
        P(("shift", "batch")),
    )
    return jax.shard_map(
        on_device,
        mesh=mesh,
        in_specs=(
            P(("shift", "batch"), None, "cols"),
            P(("shift", "batch"), "cols", None),
            P(("shift", "batch"), None),
            P(("shift", "batch"), None),
            *own,
            *own,
        ),
        out_specs=(
            P("shift", "cols"),
            P(("shift", "cols"), None),
            P("shift"),
            P("shift"),
            *own,
            *own,
        ),
        check_vma=False,
    )
```

time: 147 us -> 107 us (0.73)
  waiting for transfers between devices: 97.6 us -> 0 us
  Pallas kernels: 0 us -> 84.6 us
  blocking collectives: 20.3 us -> 0 us
  local copies, waits for them, and re-layouts: 5.93 us -> 21.1 us
  between operations: 14.6 us -> 0.78 us
  other arithmetic: 8.02 us -> 0.01 us
    pallas_call x0 -> x1, Pallas kernels: none -> 84.6 us  [on_device(): pl.pallas_call(functools.partial(kernel, n, n ** (-0.5)), out_shape=(shap...]
    reduce_scatter x2 -> x0, waiting for transfers between devices: 59.6 us -> none  [the longest x1 31.1 us: on_device(): lax.psum_scatter(partial_up[0].astype(jnp.bfloat16), 'batch', scatter_dim...]
    all_gather x2 -> x0, waiting for transfers between devices: 38 us -> none  [the longest x1 31.4 us: on_device(): lax.all_gather(stepped_down.astype(jnp.bfloat16), 'batch', axis=1, tiled=...]
    unnamed x34 -> x44, local copies, waits for them, and re-layouts: 5.93 us -> 19.9 us
    unnamed x1 -> x0, blocking collectives: 10.7 us -> none
    psum x1 -> x0, blocking collectives: 9.62 us -> none  [on_device(): lax.psum((partial_norm[0], partial_bias[0]), 'batch')]
    convert_element_type x4 -> x0, other arithmetic: 7.99 us -> none  [the longest x1 2.94 us: on_device(): partial_up[0].astype(jnp.bfloat16)]
  transfers between devices with their start and end apart: 4 -> 0, of which waited for: 4 -> 0; matrix products, arithmetic and copies ran while one was open for 5% -> 0% of each run, Pallas kernels for 0% -> 0%
where the time goes in v1:
time: 107 us; the launch traced here: 106 us
  Pallas kernels  84.6 us (79%)
  local copies, waits for them, and re-layouts  21.1 us (20%)
    pallas_call x1, Pallas kernels, on_device(): pl.pallas_call(functools.partial(kernel, n, n ** (-0.5)), out_shape=(shap...  84.6 us
    unnamed x44, local copies, waits for them, and re-layouts  19.9 us

profile of v1, /device:TPU:0, one launch (start us, length us, event | category | flops | bytes accessed | tf_op | source)
XLA Modules:
  0.0 106.5 jit_solution(7315617236292632906)
XLA Ops:
  0.6 0.0 copy-start.17
  0.7 0.0 copy-start.11
  0.7 0.0 copy-start.12
  0.7 0.0 copy-start.13
  0.7 0.0 copy-start.14
  0.7 1.4 %copy.24.md = f32[768,192]{1,0:T(8,128)S(1)} copy(f32[768,192]{0,1:T(8,128)} %param.17) | data formatting | bytes 1179648 | tf_op args[5]
  2.1 0.0 copy-done.17
  2.1 0.3 copy.25.hd
  2.4 0.0 copy-done.11
  2.4 0.0 copy-done.12
  2.4 0.0 copy-done.13
  2.4 0.0 copy-done.14
  2.4 0.0 copy-start
  2.4 1.7 %copy-done = f32[1,768,768]{2,1,0:T(8,128)S(1)} copy-done((f32[1,768,768]{2,1,0:T(8,128)S(1)}, f32[1,768,768]{2,1,0:T(8,128)}, u32[]{:S(2)}) %copy-start) | copy-done | bytes 2359320
  4.1 0.0 copy-start.1
  4.1 1.7 %copy-done.1 = f32[1,768,768]{2,1,0:T(8,128)S(1)} copy-done((f32[1,768,768]{2,1,0:T(8,128)S(1)}, f32[1,768,768]{2,1,0:T(8,128)}, u32[]{:S(2)}) %copy-start.1) | copy-done | bytes 2359320
  5.7 0.0 copy-start.5
  5.7 1.1 copy-done.5
  6.8 0.0 copy-start.6
  6.8 1.1 copy-done.6
  7.9 0.0 copy-start.15
  7.9 0.7 copy-done.15
  8.5 0.0 copy-start.16
  8.6 0.7 copy-done.16
  9.2 84.6 %shard_map.211 = (bf16[768,768]{1,0:T(8,128)(2,1)S(1)}, bf16[768,768]{1,0:T(8,128)(2,1)S(1)}, f32[2,768]{1,0:T(2,128)S(1)}, f32[192,768]{1,0:T(8,128)S(1)}, f32[...) custom-call(f32[1,768,768]{2,1,0:T(8,128)S(1)} %copy-done, ...), custom_call_target="tpu_custom_call" | custom-call | tf_op jit(solution)/shard_map/pallas_call | solution.py:251
  93.8 0.0 copy-start.2
  93.8 1.0 copy-done.2
  94.9 0.0 copy-start.4
  94.9 0.9 copy-done.4
  95.7 0.0 copy-start.7
  95.7 0.8 copy-done.7
  96.5 0.0 copy-start.9
  96.5 0.8 copy-done.9
  97.4 0.6 slice_reduce_fusion
  98.0 0.6 fusion
  98.6 0.0 copy-start.3
  98.6 2.3 %copy.26 = f32[768,192]{0,1:T(8,128)} copy(f32[768,192]{1,0:T(8,128)} %copy-done.4) | data formatting | bytes 1179648
  100.9 1.1 %copy.27 = f32[768,192]{0,1:T(8,128)} copy(f32[768,192]{1,0:T(8,128)S(1)} %get-tuple-element.39) | data formatting | bytes 1179648
  101.9 0.0 copy-done.3
  101.9 1.0 copy.32
  102.9 0.0 copy-start.10
  102.9 1.0 copy.33
  103.9 0.5 copy-done.10
  104.4 0.0 copy-start.8
  104.4 0.8 copy.34
  105.2 0.5 copy-done.8
  105.7 0.8 copy.35
  (1 shorter events, 0.0 us)
Async XLA Ops:
  0.6 1.4 %copy-start.17 = (f32[768,192]{0,1:T(8,128)S(1)}, f32[768,192]{0,1:T(8,128)}, u32[]{:S(2)}) copy-start(f32[768,192]{0,1:T(8,128)} %param.21) | copy-start | bytes 1769476
  0.7 1.7 %copy-start.11 = (f32[1,768]{1,0:T(1,128)S(1)}, f32[1,768]{1,0:T(1,128)}, u32[]{:S(2)}) copy-start(f32[1,768]{1,0:T(1,128)} %pn.1) | copy-start | bytes 9220
  0.7 1.7 %copy-start.12 = (f32[1,768]{1,0:T(1,128)S(1)}, f32[1,768]{1,0:T(1,128)}, u32[]{:S(2)}) copy-start(f32[1,768]{1,0:T(1,128)} %pb.1) | copy-start | bytes 9220
  0.7 1.7 %copy-start.13 = (f32[192]{0:T(256)S(1)}, f32[192]{0:T(256)}, u32[]{:S(2)}) copy-start(f32[192]{0:T(256)} %param.18) | copy-start | bytes 2308
  0.7 1.7 %copy-start.14 = (f32[192]{0:T(256)S(1)}, f32[192]{0:T(256)}, u32[]{:S(2)}) copy-start(f32[192]{0:T(256)} %param.19) | copy-start | bytes 2308
  2.4 1.7 %copy-start = (f32[1,768,768]{2,1,0:T(8,128)S(1)}, f32[1,768,768]{2,1,0:T(8,128)}, u32[]{:S(2)}) copy-start(f32[1,768,768]{2,1,0:T(8,128)} %pu.1) | copy-start | bytes 7077892
  4.1 1.7 %copy-start.1 = (f32[1,768,768]{2,1,0:T(8,128)S(1)}, f32[1,768,768]{2,1,0:T(8,128)}, u32[]{:S(2)}) copy-start(f32[1,768,768]{2,1,0:T(8,128)} %pd.1) | copy-start | bytes 7077892
  5.7 1.1 copy-start.5
  6.8 1.1 copy-start.6
  7.9 0.7 copy-start.15
  8.5 0.7 copy-start.16
  93.8 1.0 copy-start.2
  94.9 0.9 copy-start.4
  95.7 0.8 copy-start.7
  96.5 0.8 copy-start.9
  98.6 3.4 %copy-start.3 = (bf16[768,768]{1,0:T(8,128)(2,1)S(1)}, bf16[768,768]{1,0:T(8,128)(2,1)}, u32[]{:S(2)}) copy-start(bf16[768,768]{1,0:T(8,128)(2,1)} %copy-done.2) | copy-start | bytes 3538948
  102.9 1.5 %copy-start.10 = (f32[192,768]{1,0:T(8,128)S(1)}, f32[192,768]{1,0:T(8,128)}, u32[]{:S(2)}) copy-start(f32[192,768]{1,0:T(8,128)} %copy-done.9) | copy-start | bytes 1769476
  104.4 1.3 %copy-start.8 = (f32[192,768]{1,0:T(8,128)S(1)}, f32[192,768]{1,0:T(8,128)}, u32[]{:S(2)}) copy-start(f32[192,768]{1,0:T(8,128)} %copy-done.7) | copy-start | bytes 1769476

commit v2 on v0

v2 whole, which is shorter than its diff:
```python
import functools

import jax
import jax.numpy as jnp
from jax import lax
from jax.experimental import pallas as pl
from jax.experimental.pallas import tpu as pltpu
from jax.sharding import PartitionSpec as P

learn_rate = 0.1
hold_rate = 0.8
bf16, f32 = jnp.bfloat16, jnp.float32
MESH = pl.DeviceIdType.MESH
RIGHT, LEFT = 0, 1
CHUNK = 256
MOST = 67043328
LEAD = 1
LAG = 1


def line_kernel(
    n, rate,
    pu, pd, pn, pb, mu, md, mn, mb, hu, hd, hn, hb,
    cu, cd, cn, cb, su, sd, sn, sb, tu, td, tn, tb,
    vpu, vpd, vmu, vmd, vhu, vhd, vpn, vpb, vmn, vmb, vhn, vhb,
    send, got, acc, vs, vr, vg,
    in_sem, rs_send, rs_recv, ag_send, ag_recv, vec_send, vec_recv,
):
    me = lax.axis_index("batch")
    size, width = vpu.shape
    w = size // n
    per = width // CHUNK
    count = 2 * per
    first, last = me == 0, me == n - 1
    mine = pl.ds(pl.multiple_of(me * w, w), w)
    toward = ({"batch": jnp.minimum(me + 1, n - 1)}, {"batch": jnp.maximum(me - 1, 0)})

    loads = {}

    def load(name, src, dst):
        copy = pltpu.make_async_copy(src, dst, in_sem.at[len(loads)])
        copy.start()
        loads[name] = copy

    def lanes(q):
        return slice((q % per) * CHUNK, (q % per + 1) * CHUNK)

    def load_chunk(q):
        if q < per:
            load(q, pu.at[0, :, lanes(q)], vpu.at[:, lanes(q)])
        else:
            load(q, pd.at[0, lanes(q), :], vpd.at[lanes(q), :])

    for q in range(2):
        load_chunk(q)
    vectors = ((pn, vpn), (pb, vpb), (mn, vmn), (mb, vmb), (hn, vhn), (hb, vhb))
    for i, (src, dst) in enumerate(vectors):
        load(("vector", i), src, dst)
    load("mu", mu, vmu)
    load("hu", hu, vhu)
    for q in range(2, count):
        load_chunk(q)
    load("md", md, vmd)
    load("hd", hd, vhd)

    def at(d):
        return lax.rem(me + d + n, n)

    barrier = pltpu.get_barrier_semaphore()
    for d in range(1, n):
        pl.semaphore_signal(barrier, inc=1, device_id={"batch": at(d)}, device_id_type=MESH)

    def pack(q):
        loads[q].wait()
        if q < per:
            send[0, :, lanes(q)] = vpu[:, lanes(q)].astype(bf16)
        else:
            send[1, :, lanes(q)] = vpd[lanes(q), :].T.astype(bf16)

    def scatter(side, q, j):
        here = (q // per, slice(j * w, (j + 1) * w), lanes(q))
        return pltpu.make_async_remote_copy(
            src_ref=send.at[here],
            dst_ref=got.at[(side, *here)],
            send_sem=rs_send.at[side, q, j],
            recv_sem=rs_recv.at[side, q, j],
            device_id=toward[side],
            device_id_type=MESH,
        )

    def gather(side, q, j):
        out = (cu, cd)[q // per].at[pl.ds(pl.multiple_of(j * w, w), w), lanes(q)]
        return pltpu.make_async_remote_copy(
            src_ref=out,
            dst_ref=out,
            send_sem=ag_send.at[side, q, j],
            recv_sem=ag_recv.at[side, q, j],
            device_id=toward[side],
            device_id_type=MESH,
        )

    def vector(phase, d, src, dst):
        return pltpu.make_async_remote_copy(
            src_ref=src,
            dst_ref=dst,
            send_sem=vec_send.at[phase, d],
            recv_sem=vec_recv.at[phase, d],
            device_id={"batch": at(d)},
            device_id_type=MESH,
        )

    def add(side, q, j):
        here = (q // per, slice(j * w, (j + 1) * w), lanes(q))
        send[here] = (send[here].astype(f32) + got[(side, *here)].astype(f32)).astype(bf16)

    def start_ends(q):
        @pl.when(first)
        def _():
            for j in range(n - 1, 0, -1):
                scatter(RIGHT, q, j).start()

        @pl.when(last)
        def _():
            for j in range(n - 1):
                scatter(LEFT, q, j).start()

    def reduce(q):
        for s in range(n - 1):
            j = n - 1 - s

            @pl.when(jnp.logical_and(me > 0, me <= j))
            def _():
                scatter(RIGHT, q, j).wait_recv()

            @pl.when(jnp.logical_and(me > 0, me < j))
            def _():
                add(RIGHT, q, j)
                scatter(RIGHT, q, j).start()

            @pl.when(jnp.logical_and(me < n - 1, me >= s))
            def _():
                scatter(LEFT, q, s).wait_recv()

            @pl.when(jnp.logical_and(me < n - 1, me > s))
            def _():
                add(LEFT, q, s)
                scatter(LEFT, q, s).start()

    def update(q):
        m, cut = q // per, lanes(q)
        acc[...] = send[m, mine, cut].astype(f32)

        @pl.when(me > 0)
        def _():
            acc[...] += got[RIGHT, m, mine, cut].astype(f32)

        @pl.when(me < n - 1)
        def _():
            acc[...] += got[LEFT, m, mine, cut].astype(f32)

        if q % per == 0:
            loads[("mu", "md")[m]].wait()
            loads[("hu", "hd")[m]].wait()
        state = hold_rate * (vhu, vhd)[m][:, cut] + acc[...] * rate
        stepped = (vmu, vmd)[m][:, cut] - learn_rate * state
        (cu, cd)[m][mine, cut] = stepped.astype(bf16)

        @pl.when(me < n - 1)
        def _():
            gather(RIGHT, q, me).start()

        @pl.when(me > 0)
        def _():
            gather(LEFT, q, me).start()

        (tu, td)[m][:, cut] = state
        (su, sd)[m][:, cut] = stepped

    def forward(q):
        for e in range(1, n):
            @pl.when(me - e >= 0)
            def _():
                gather(RIGHT, q, me - e).wait_recv()

            @pl.when(jnp.logical_and(me - e >= 0, me < n - 1))
            def _():
                gather(RIGHT, q, me - e).start()

            @pl.when(me + e < n)
            def _():
                gather(LEFT, q, me + e).wait_recv()

            @pl.when(jnp.logical_and(me + e < n, me > 0))
            def _():
                gather(LEFT, q, me + e).start()

    pack(0)
    pl.semaphore_wait(barrier, n - 1)
    start_ends(0)
    for q in range(1, LEAD):
        pack(q)
        start_ends(q)
    for i in range(len(vectors)):
        loads["vector", i].wait()
    for k in range(n):
        vs[k, 0:1, :] = vpn[:, k * w : (k + 1) * w]
        vs[k, 1:2, :] = vpb[:, k * w : (k + 1) * w]
    for d in range(1, n):
        vector(0, d, vs.at[at(d)], vr.at[d]).start()

    for t in range(count + LAG):
        if t + LEAD < count:
            pack(t + LEAD)
            start_ends(t + LEAD)
        if t < count:
            reduce(t)
            update(t)
        if t == 1:
            total = vs[me]
            for d in range(1, n):
                vector(0, d, vs.at[at(d)], vr.at[d]).wait_recv()
                total = total + vr[d]
            for i, (m, h, s, o) in enumerate(((vmn, vhn, tn, sn), (vmb, vhb, tb, sb))):
                state = hold_rate * h[...] + total[i : i + 1] * rate
                stepped = m[...] - learn_rate * state
                s[...] = state
                o[...] = stepped
                vg[me, i : i + 1, :] = stepped
            for d in range(1, n):
                vector(1, d, vg.at[me], vg.at[me]).start()
        if t == 2:
            for e in range(1, n):
                vector(1, e, vg.at[at(-e)], vg.at[at(-e)]).wait_recv()
            for k in range(n):
                cn[:, k * w : (k + 1) * w] = vg[k, 0:1, :]
                cb[:, k * w : (k + 1) * w] = vg[k, 1:2, :]
        if t >= LAG:
            forward(t - LAG)

    for q in range(count):
        for j in range(n):
            @pl.when(me < j)
            def _():
                scatter(RIGHT, q, j).wait_send()

            @pl.when(me > j)
            def _():
                scatter(LEFT, q, j).wait_send()

            @pl.when(jnp.logical_and(me >= j, me < n - 1))
            def _():
                gather(RIGHT, q, j).wait_send()

            @pl.when(jnp.logical_and(me <= j, me > 0))
            def _():
                gather(LEFT, q, j).wait_send()
    for d in range(1, n):
        vector(0, d, vs.at[at(d)], vr.at[d]).wait_send()
        vector(1, d, vg.at[me], vg.at[me]).wait_send()


def write_kernel(
    cu, cd, cn, cb, su, sd, sn, sb, tu, td, tn, tb,
    ocu, ocd, ocn, ocb, osu, osd, osn, osb, otu, otd, otn, otb,
    vcd, sem,
):
    copies = [
        pltpu.make_async_copy(src, dst, sem.at[i])
        for i, (src, dst) in enumerate(((cu, ocu), (su, osu), (sd, osd), (tu, otu), (td, otd)))
    ]
    for copy in copies:
        copy.start()
    rows = vcd.shape[0]
    strip = rows // 3
    for i in range(3):
        r = slice(i * strip, (i + 1) * strip)
        vcd[r, :] = cd[:, r].astype(f32).T.astype(bf16)
        copies.append(pltpu.make_async_copy(vcd.at[r, :], ocd.at[r, :], sem.at[5 + i]))
        copies[-1].start()
    ocn[...] = cn[...].astype(bf16)
    ocb[...] = cb[...].astype(bf16)
    for src, dst in ((sn, osn), (sb, osb), (tn, otn), (tb, otb)):
        dst[...] = src[...]
    for copy in copies:
        copy.wait()


def on_device(pu, pd, pn, pb, mu, md, mn, mb, hu, hd, hn, hb):
    n = lax.axis_size("batch")
    size, width = pu.shape[1:]
    w = size // n
    count = 2 * width // CHUNK
    line = lambda v: v.reshape(1, -1)
    shape = jax.ShapeDtypeStruct
    vmem = pl.BlockSpec(memory_space=pltpu.VMEM)
    hbm = pl.BlockSpec(memory_space=pltpu.HBM)
    dma = pltpu.SemaphoreType.DMA
    whole, share = (size, width), (w, width)
    row, part = (1, size), (1, w)
    owned = (shape(share, f32), shape(share, f32), shape(part, f32), shape(part, f32))
    results = pl.pallas_call(
        functools.partial(line_kernel, n, n ** (-0.5)),
        out_shape=(
            shape(whole, bf16), shape(whole, bf16), shape(row, f32), shape(row, f32),
            *owned, *owned,
        ),
        in_specs=(hbm,) * 12,
        out_specs=(vmem,) * 12,
        scratch_shapes=[
            pltpu.VMEM(whole, f32),
            pltpu.VMEM(whole, f32),
            *[pltpu.VMEM(share, f32)] * 4,
            *[pltpu.VMEM(row, f32)] * 2,
            *[pltpu.VMEM(part, f32)] * 4,
            pltpu.VMEM((2, *whole), bf16),
            pltpu.VMEM((2, 2, *whole), bf16),
            pltpu.VMEM((w, CHUNK), f32),
            *[pltpu.VMEM((n, 2, w), f32)] * 3,
            dma((count + 10,)),
            *[dma((2, count, n))] * 4,
            *[dma((2, n))] * 2,
        ],
        compiler_params=pltpu.CompilerParams(
            collective_id=0, has_side_effects=True, vmem_limit_bytes=MOST
        ),
    )(pu, pd, pn, pb, mu, md.T, line(mn), line(mb), hu, hd.T, line(hn), line(hb))
    cu, cd, cn, cb, su, sd, sn, sb, tu, td, tn, tb = pl.pallas_call(
        write_kernel,
        out_shape=(
            shape(whole, bf16), shape(whole, bf16), shape(row, bf16), shape(row, bf16),
            *owned, *owned,
        ),
        in_specs=(vmem,) * 12,
        out_specs=(hbm, hbm, vmem, vmem) * 3,
        scratch_shapes=[pltpu.VMEM(whole, bf16), dma((8,))],
        compiler_params=pltpu.CompilerParams(vmem_limit_bytes=MOST),
    )(*results)
    flat = lambda v: v.reshape(-1)
    return (
        cu, cd, flat(cn), flat(cb),
        su, sd.T, flat(sn), flat(sb),
        tu, td.T, flat(tn), flat(tb),
    )


def solution(mesh):
    own = (
        P(("shift", "batch"), "cols"),
        P(("shift", "cols"), "batch"),
        P(("shift", "batch")),
        P(("shift", "batch")),
    )
    return jax.shard_map(
        on_device,
        mesh=mesh,
        in_specs=(
            P(("shift", "batch"), None, "cols"),
            P(("shift", "batch"), "cols", None),
            P(("shift", "batch"), None),
            P(("shift", "batch"), None),
            *own,
            *own,
        ),
        out_specs=(
            P("shift", "cols"),
            P(("shift", "cols"), None),
            P("shift"),
            P("shift"),
            *own,
            *own,
        ),
        check_vma=False,
    )
```

time: 147 us -> 143 us (0.973)
  Pallas kernels: 0 us -> 140 us
  waiting for transfers between devices: 97.6 us -> 0 us
  blocking collectives: 20.3 us -> 0 us
  between operations: 14.6 us -> 0.67 us
  local copies, waits for them, and re-layouts: 5.93 us -> 0 us
  other arithmetic: 8.02 us -> 2.54 us
    pallas_call x0 -> x2, Pallas kernels: none -> 140 us  [the longest x1 135 us: on_device(): pl.pallas_call(functools.partial(line_kernel, n, n ** (-0.5)), out_shape=...]
    reduce_scatter x2 -> x0, waiting for transfers between devices: 59.6 us -> none  [the longest x1 31.1 us: on_device(): lax.psum_scatter(partial_up[0].astype(jnp.bfloat16), 'batch', scatter_dim...]
    all_gather x2 -> x0, waiting for transfers between devices: 38 us -> none  [the longest x1 31.4 us: on_device(): lax.all_gather(stepped_down.astype(jnp.bfloat16), 'batch', axis=1, tiled=...]
    unnamed x1 -> x0, blocking collectives: 10.7 us -> none
    psum x1 -> x0, blocking collectives: 9.62 us -> none  [on_device(): lax.psum((partial_norm[0], partial_bias[0]), 'batch')]
    convert_element_type x4 -> x0, other arithmetic: 7.99 us -> none  [the longest x1 2.94 us: on_device(): partial_up[0].astype(jnp.bfloat16)]
    unnamed x34 -> x0, local copies, waits for them, and re-layouts: 5.93 us -> none
    pallas_call x0 -> x2, other arithmetic: none -> 2.54 us  [on_device(): pl.pallas_call(write_kernel, out_shape=(shape(whole, bf16), shape(whole,...]
  transfers between devices with their start and end apart: 4 -> 0, of which waited for: 4 -> 0; matrix products, arithmetic and copies ran while one was open for 5% -> 0% of each run, Pallas kernels for 0% -> 0%
where the time goes in v2:
time: 143 us
  Pallas kernels  140 us (98%)
  other arithmetic  2.54 us (2%)
    pallas_call x1, Pallas kernels, on_device(): pl.pallas_call(functools.partial(line_kernel, n, n ** (-0.5)), out_shape=...  135 us
    pallas_call x1, Pallas kernels, on_device(): pl.pallas_call(write_kernel, out_shape=(shape(whole, bf16), shape(whole,...  5.18 us

profile of v2, /device:TPU:0, one launch (start us, length us, event | category | flops | bytes accessed | tf_op | source)
XLA Modules:
  0.0 143.1 jit_solution(17227720711689031960)
XLA Ops:
  0.6 134.7 %shard_map.211 = (bf16[768,768]{1,0:T(8,128)(2,1)}, bf16[768,768]{1,0:T(8,128)(2,1)}, f32[1,768]{1,0:T(1,128)}, f32[1,768]{1,0:T(1,128)}, f32[192,768]{1,0:T(8,1...) custom-call(f32[1,768,768]{2,1,0:T(8,128)} %pu.1, ...), custom_call_target="tpu_custom_call" | custom-call | tf_op jit(solution)/shard_map/pallas_call | solution.py:301
  135.4 5.2 %shard_map.212 = (bf16[768,768]{1,0:T(8,128)(2,1)}, bf16[768,768]{1,0:T(8,128)(2,1)}, bf16[1,768]{1,0:T(2,128)(2,1)}, bf16[1,768]{1,0:T(2,128)(2,1)}, f32[192,76...) custom-call(bf16[768,768]{1,0:T(8,128)(2,1)} %get-tuple-element.36.c, ...), custom_call_target="tpu_custom_call" | custom-call | tf_op jit(solution)/shard_map/pallas_call | solution.py:327
  140.6 1.3 reduce
  141.8 1.3 reduce.1

commit v3 on v2

--- a/solution.py
+++ b/solution.py
@@ -12,10 +12,8 @@
 bf16, f32 = jnp.bfloat16, jnp.float32
 MESH = pl.DeviceIdType.MESH
 RIGHT, LEFT = 0, 1
-CHUNK = 256
+SUBS = 3
 MOST = 67043328
-LEAD = 1
-LAG = 1
 
 
 def line_kernel(
@@ -29,10 +27,10 @@
     me = lax.axis_index("batch")
     size, width = vpu.shape
     w = size // n
-    per = width // CHUNK
+    per = SUBS
     count = 2 * per
+    r = w // per
     first, last = me == 0, me == n - 1
-    mine = pl.ds(pl.multiple_of(me * w, w), w)
     toward = ({"batch": jnp.minimum(me + 1, n - 1)}, {"batch": jnp.maximum(me - 1, 0)})
 
     loads = {}
@@ -42,24 +40,27 @@
         copy.start()
         loads[name] = copy
 
-    def lanes(q):
-        return slice((q % per) * CHUNK, (q % per + 1) * CHUNK)
-
-    def load_chunk(q):
-        if q < per:
-            load(q, pu.at[0, :, lanes(q)], vpu.at[:, lanes(q)])
-        else:
-            load(q, pd.at[0, lanes(q), :], vpd.at[lanes(q), :])
-
-    for q in range(2):
-        load_chunk(q)
+    def rows(q, j):
+        if isinstance(j, int):
+            return pl.ds(j * w + q % per * r, r)
+        return pl.ds(pl.multiple_of(j * w + q % per * r, r), r)
+
+    def part(q):
+        return pl.ds(q % per * r, r)
+
+    def load_up(q):
+        for j in range(n):
+            load((q, j), pu.at[0, rows(q, j), :], vpu.at[rows(q, j), :])
+
+    load_up(0)
+    load("down", pd.at[0], vpd)
     vectors = ((pn, vpn), (pb, vpb), (mn, vmn), (mb, vmb), (hn, vhn), (hb, vhb))
     for i, (src, dst) in enumerate(vectors):
         load(("vector", i), src, dst)
     load("mu", mu, vmu)
     load("hu", hu, vhu)
-    for q in range(2, count):
-        load_chunk(q)
+    for q in range(1, per):
+        load_up(q)
     load("md", md, vmd)
     load("hd", hd, vhd)
 
@@ -71,14 +72,19 @@
         pl.semaphore_signal(barrier, inc=1, device_id={"batch": at(d)}, device_id_type=MESH)
 
     def pack(q):
-        loads[q].wait()
         if q < per:
-            send[0, :, lanes(q)] = vpu[:, lanes(q)].astype(bf16)
-        else:
-            send[1, :, lanes(q)] = vpd[lanes(q), :].T.astype(bf16)
+            for j in range(n):
+                loads[q, j].wait()
+                send[0, rows(q, j), :] = vpu[rows(q, j), :].astype(bf16)
+        elif q == per:
+            loads["down"].wait()
+            strip = width // 3
+            for i in range(3):
+                cut = slice(i * strip, (i + 1) * strip)
+                send[1, :, cut] = vpd[cut, :].T.astype(bf16)
 
     def scatter(side, q, j):
-        here = (q // per, slice(j * w, (j + 1) * w), lanes(q))
+        here = (q // per, rows(q, j))
         return pltpu.make_async_remote_copy(
             src_ref=send.at[here],
             dst_ref=got.at[(side, *here)],
@@ -89,7 +95,7 @@
         )
 
     def gather(side, q, j):
-        out = (cu, cd)[q // per].at[pl.ds(pl.multiple_of(j * w, w), w), lanes(q)]
+        out = (cu, cd)[q // per].at[rows(q, j)]
         return pltpu.make_async_remote_copy(
             src_ref=out,
             dst_ref=out,
@@ -110,7 +116,7 @@
         )
 
     def add(side, q, j):
-        here = (q // per, slice(j * w, (j + 1) * w), lanes(q))
+        here = (q // per, rows(q, j))
         send[here] = (send[here].astype(f32) + got[(side, *here)].astype(f32)).astype(bf16)
 
     def start_ends(q):
@@ -124,46 +130,29 @@
             for j in range(n - 1):
                 scatter(LEFT, q, j).start()
 
-    def reduce(q):
-        for s in range(n - 1):
-            j = n - 1 - s
-
-            @pl.when(jnp.logical_and(me > 0, me <= j))
-            def _():
-                scatter(RIGHT, q, j).wait_recv()
-
-            @pl.when(jnp.logical_and(me > 0, me < j))
-            def _():
-                add(RIGHT, q, j)
-                scatter(RIGHT, q, j).start()
-
-            @pl.when(jnp.logical_and(me < n - 1, me >= s))
-            def _():
-                scatter(LEFT, q, s).wait_recv()
-
-            @pl.when(jnp.logical_and(me < n - 1, me > s))
-            def _():
-                add(LEFT, q, s)
-                scatter(LEFT, q, s).start()
+    def reduce(side, q, i):
+        blocks = range(n - 1, i - 1, -1) if side == RIGHT else range(i + 1)
+        for j in blocks:
+            scatter(side, q, j).wait_recv()
+            if j != i:
+                add(side, q, j)
+                scatter(side, q, j).start()
 
     def update(q):
-        m, cut = q // per, lanes(q)
-        acc[...] = send[m, mine, cut].astype(f32)
+        m, own, cut = q // per, rows(q, me), part(q)
+        acc[...] = send[m, own].astype(f32)
 
         @pl.when(me > 0)
         def _():
-            acc[...] += got[RIGHT, m, mine, cut].astype(f32)
+            acc[...] += got[RIGHT, m, own].astype(f32)
 
         @pl.when(me < n - 1)
         def _():
-            acc[...] += got[LEFT, m, mine, cut].astype(f32)
-
-        if q % per == 0:
-            loads[("mu", "md")[m]].wait()
-            loads[("hu", "hd")[m]].wait()
-        state = hold_rate * (vhu, vhd)[m][:, cut] + acc[...] * rate
-        stepped = (vmu, vmd)[m][:, cut] - learn_rate * state
-        (cu, cd)[m][mine, cut] = stepped.astype(bf16)
+            acc[...] += got[LEFT, m, own].astype(f32)
+
+        state = hold_rate * (vhu, vhd)[m][cut, :] + acc[...] * rate
+        stepped = (vmu, vmd)[m][cut, :] - learn_rate * state
+        (cu, cd)[m][own, :] = stepped.astype(bf16)
 
         @pl.when(me < n - 1)
         def _():
@@ -173,33 +162,35 @@
         def _():
             gather(LEFT, q, me).start()
 
-        (tu, td)[m][:, cut] = state
-        (su, sd)[m][:, cut] = stepped
-
-    def forward(q):
-        for e in range(1, n):
-            @pl.when(me - e >= 0)
-            def _():
-                gather(RIGHT, q, me - e).wait_recv()
-
-            @pl.when(jnp.logical_and(me - e >= 0, me < n - 1))
-            def _():
-                gather(RIGHT, q, me - e).start()
-
-            @pl.when(me + e < n)
-            def _():
-                gather(LEFT, q, me + e).wait_recv()
-
-            @pl.when(jnp.logical_and(me + e < n, me > 0))
-            def _():
-                gather(LEFT, q, me + e).start()
+        (tu, td)[m][cut, :] = state
+        (su, sd)[m][cut, :] = stepped
+
+    def forward(side, q, i, j):
+        gather(side, q, j).wait_recv()
+        if i != (n - 1 if side == RIGHT else 0):
+            gather(side, q, j).start()
+
+    def hop(q, d):
+        for i in range(n):
+            tasks = []
+            if d == i > 0:
+                tasks.append(functools.partial(reduce, RIGHT, q, i))
+            if d == n - 1 - i > 0:
+                tasks.append(functools.partial(reduce, LEFT, q, i))
+            if d == max(i, n - 1 - i):
+                tasks.append(functools.partial(update, q))
+            for j in range(n):
+                if j != i and d == max(j, n - 1 - j) + abs(i - j):
+                    tasks.append(functools.partial(forward, RIGHT if j < i else LEFT, q, i, j))
+            if tasks:
+                @pl.when(me == i)
+                def _():
+                    for task in tasks:
+                        task()
 
     pack(0)
     pl.semaphore_wait(barrier, n - 1)
     start_ends(0)
-    for q in range(1, LEAD):
-        pack(q)
-        start_ends(q)
     for i in range(len(vectors)):
         loads["vector", i].wait()
     for k in range(n):
@@ -208,14 +199,16 @@
     for d in range(1, n):
         vector(0, d, vs.at[at(d)], vr.at[d]).start()
 
-    for t in range(count + LAG):
-        if t + LEAD < count:
-            pack(t + LEAD)
-            start_ends(t + LEAD)
+    for t in range(1, count + 2 * n - 2):
         if t < count:
-            reduce(t)
-            update(t)
+            pack(t)
+            start_ends(t)
         if t == 1:
+            for name in ("mu", "hu", "md", "hd"):
+                loads[name].wait()
+        for q in range(count):
+            hop(q, t - q)
+        if t == 2:
             total = vs[me]
             for d in range(1, n):
                 vector(0, d, vs.at[at(d)], vr.at[d]).wait_recv()
@@ -228,14 +221,12 @@
                 vg[me, i : i + 1, :] = stepped
             for d in range(1, n):
                 vector(1, d, vg.at[me], vg.at[me]).start()
-        if t == 2:
+        if t == 3:
             for e in range(1, n):
                 vector(1, e, vg.at[at(-e)], vg.at[at(-e)]).wait_recv()
             for k in range(n):
                 cn[:, k * w : (k + 1) * w] = vg[k, 0:1, :]
                 cb[:, k * w : (k + 1) * w] = vg[k, 1:2, :]
-        if t >= LAG:
-            forward(t - LAG)
 
     for q in range(count):
         for j in range(n):
@@ -289,7 +280,7 @@
     n = lax.axis_size("batch")
     size, width = pu.shape[1:]
     w = size // n
-    count = 2 * width // CHUNK
+    count = 2 * SUBS
     line = lambda v: v.reshape(1, -1)
     shape = jax.ShapeDtypeStruct
     vmem = pl.BlockSpec(memory_space=pltpu.VMEM)
@@ -314,9 +305,9 @@
             *[pltpu.VMEM(part, f32)] * 4,
             pltpu.VMEM((2, *whole), bf16),
             pltpu.VMEM((2, 2, *whole), bf16),
-            pltpu.VMEM((w, CHUNK), f32),
+            pltpu.VMEM((w // SUBS, width), f32),
             *[pltpu.VMEM((n, 2, w), f32)] * 3,
-            dma((count + 10,)),
+            dma((SUBS * n + 11,)),
             *[dma((2, count, n))] * 4,
             *[dma((2, n))] * 2,
         ],

time: 143 us -> 90.5 us (0.63)
  Pallas kernels: 140 us -> 87.1 us
    pallas_call x1, Pallas kernels: 135 us -> 81.9 us  [on_device(): pl.pallas_call(functools.partial(line_kernel, n, n ** (-0.5)), out_shape=...]
where the time goes in v3:
time: 90.5 us; the launch traced here: 90.3 us
  Pallas kernels  87.1 us (96%)
  other arithmetic  2.54 us (3%)
    pallas_call x1, Pallas kernels, on_device(): pl.pallas_call(functools.partial(line_kernel, n, n ** (-0.5)), out_shape=...  81.9 us
    pallas_call x1, Pallas kernels, on_device(): pl.pallas_call(write_kernel, out_shape=(shape(whole, bf16), shape(whole,...  5.18 us
    pallas_call x2, other arithmetic, on_device(): pl.pallas_call(write_kernel, out_shape=(shape(whole, bf16), shape(whole,...  2.54 us

profile of v3, /device:TPU:0, one launch (start us, length us, event | category | flops | bytes accessed | tf_op | source)
XLA Modules:
  0.0 90.3 jit_solution(9576331281306456752)
XLA Ops:
  0.6 81.9 %shard_map.211 = (bf16[768,768]{1,0:T(8,128)(2,1)}, bf16[768,768]{1,0:T(8,128)(2,1)}, f32[1,768]{1,0:T(1,128)}, f32[1,768]{1,0:T(1,128)}, f32[192,768]{1,0:T(8,1...) custom-call(f32[1,768,768]{2,1,0:T(8,128)} %pu.1, ...), custom_call_target="tpu_custom_call" | custom-call | tf_op jit(solution)/shard_map/pallas_call | solution.py:292
  82.6 5.2 %shard_map.212 = (bf16[768,768]{1,0:T(8,128)(2,1)}, bf16[768,768]{1,0:T(8,128)(2,1)}, bf16[1,768]{1,0:T(2,128)(2,1)}, bf16[1,768]{1,0:T(2,128)(2,1)}, f32[192,76...) custom-call(bf16[768,768]{1,0:T(8,128)(2,1)} %get-tuple-element.36.c, ...), custom_call_target="tpu_custom_call" | custom-call | tf_op jit(solution)/shard_map/pallas_call | solution.py:318
  87.7 1.3 %reduce = bf16[768]{0:T(1024)(128)(2,1)} reduce(bf16[1,768]{1,0:T(2,128)(2,1)} %get-tuple-element.50, bf16[]{:T(256)} %constant.4), dimensions={0}, to_apply=%get-tuple-element.50.reduce_sub_computation | reduce | bytes 3074 | tf_op jit(solution)/shard_map/pallas_call | solution.py:318
  89.0 1.3 %reduce.1 = bf16[768]{0:T(1024)(128)(2,1)} reduce(bf16[1,768]{1,0:T(2,128)(2,1)} %get-tuple-element.51, bf16[]{:T(256)} %constant.4), dimensions={0}, to_apply=%get-tuple-element.51.reduce_sub_computation | reduce | bytes 3074 | tf_op jit(solution)/shard_map/pallas_call | solution.py:318

commit v4 on v3

--- a/solution.py
+++ b/solution.py
@@ -13,6 +13,7 @@
 MESH = pl.DeviceIdType.MESH
 RIGHT, LEFT = 0, 1
 SUBS = 3
+SKEW = 2
 MOST = 67043328
 
 
@@ -173,14 +174,14 @@
     def hop(q, d):
         for i in range(n):
             tasks = []
-            if d == i > 0:
+            if i > 0 and d == SKEW * i:
                 tasks.append(functools.partial(reduce, RIGHT, q, i))
-            if d == n - 1 - i > 0:
+            if i < n - 1 and d == SKEW * (n - 1 - i):
                 tasks.append(functools.partial(reduce, LEFT, q, i))
-            if d == max(i, n - 1 - i):
+            if d == SKEW * max(i, n - 1 - i):
                 tasks.append(functools.partial(update, q))
             for j in range(n):
-                if j != i and d == max(j, n - 1 - j) + abs(i - j):
+                if j != i and d == SKEW * (max(j, n - 1 - j) + abs(i - j)):
                     tasks.append(functools.partial(forward, RIGHT if j < i else LEFT, q, i, j))
             if tasks:
                 @pl.when(me == i)
@@ -199,7 +200,7 @@
     for d in range(1, n):
         vector(0, d, vs.at[at(d)], vr.at[d]).start()
 
-    for t in range(1, count + 2 * n - 2):
+    for t in range(1, count + SKEW * (2 * n - 2)):
         if t < count:
             pack(t)
             start_ends(t)
@@ -268,8 +269,8 @@
         vcd[r, :] = cd[:, r].astype(f32).T.astype(bf16)
         copies.append(pltpu.make_async_copy(vcd.at[r, :], ocd.at[r, :], sem.at[5 + i]))
         copies[-1].start()
-    ocn[...] = cn[...].astype(bf16)
-    ocb[...] = cb[...].astype(bf16)
+    ocn[...] = cn[...]
+    ocb[...] = cb[...]
     for src, dst in ((sn, osn), (sb, osb), (tn, otn), (tb, otb)):
         dst[...] = src[...]
     for copy in copies:
@@ -318,7 +319,7 @@
     cu, cd, cn, cb, su, sd, sn, sb, tu, td, tn, tb = pl.pallas_call(
         write_kernel,
         out_shape=(
-            shape(whole, bf16), shape(whole, bf16), shape(row, bf16), shape(row, bf16),
+            shape(whole, bf16), shape(whole, bf16), shape(row, f32), shape(row, f32),
             *owned, *owned,
         ),
         in_specs=(vmem,) * 12,
@@ -328,7 +329,7 @@
     )(*results)
     flat = lambda v: v.reshape(-1)
     return (
-        cu, cd, flat(cn), flat(cb),
+        cu, cd, flat(cn).astype(bf16), flat(cb).astype(bf16),
         su, sd.T, flat(sn), flat(sb),
         tu, td.T, flat(tn), flat(tb),
     )

time: 90.5 us -> 88.9 us (0.982)
  other arithmetic: 2.54 us -> 1.28 us
    pallas_call x2 -> x0, other arithmetic: 2.54 us -> none  [on_device(): pl.pallas_call(write_kernel, out_shape=(shape(whole, bf16), shape(whole,...]
    convert_element_type x0 -> x1, other arithmetic: none -> 1.28 us  [on_device(): flat(cb).astype(bf16)]
where the time goes in v4:
time: 88.9 us; the launch traced here: 88.7 us
  Pallas kernels  86.8 us (98%)
  other arithmetic  1.28 us (1%)
    pallas_call x1, Pallas kernels, on_device(): pl.pallas_call(functools.partial(line_kernel, n, n ** (-0.5)), out_shape=...  81.6 us
    pallas_call x1, Pallas kernels, on_device(): pl.pallas_call(write_kernel, out_shape=(shape(whole, bf16), shape(whole,...  5.18 us

profile of v4, /device:TPU:0, one launch (start us, length us, event | category | flops | bytes accessed | tf_op | source)
XLA Modules:
  0.0 88.7 jit_solution(5828436829950596919)
XLA Ops:
  0.6 81.6 %shard_map.211 = (bf16[768,768]{1,0:T(8,128)(2,1)}, bf16[768,768]{1,0:T(8,128)(2,1)}, f32[1,768]{1,0:T(1,128)}, f32[1,768]{1,0:T(1,128)}, f32[192,768]{1,0:T(8,1...) custom-call(f32[1,768,768]{2,1,0:T(8,128)} %pu.1, ...), custom_call_target="tpu_custom_call" | custom-call | tf_op jit(solution)/shard_map/pallas_call | solution.py:293
  82.3 5.2 %shard_map.212 = (bf16[768,768]{1,0:T(8,128)(2,1)}, bf16[768,768]{1,0:T(8,128)(2,1)}, f32[1,768]{1,0:T(1,128)}, f32[1,768]{1,0:T(1,128)}, f32[192,768]{1,0:T(8,1...) custom-call(bf16[768,768]{1,0:T(8,128)(2,1)} %get-tuple-element.36.c, ...), custom_call_target="tpu_custom_call" | custom-call | tf_op jit(solution)/shard_map/pallas_call | solution.py:319
  87.4 1.3 %convert_reduce_fusion = (bf16[768]{0:T(1024)(128)(2,1)}, bf16[768]{0:T(1024)(128)(2,1)}) fusion(f32[1,768]{1,0:T(1,128)} %get-tuple-element.51, f32[1,768]{1,0:T(1,128)} %get-tuple-element.50), kind=kLoop, calls=%fused_computation | loop fusion | flops 1536 | bytes 9216 | tf_op jit(solution)/shard_map/convert_element_type | solution.py:332
